TPU v7x, 32 devices: a whole 2x2x4 slice. The times are simulated.
32 devices in a mesh: grp: 4 (over y, x), dev: 8 (over z, core).
Axes of the slice: x: 2, y: 2, z: 4, core: 2. Of those that a mesh axis runs over, the one named last changes fastest.
Arguments:
- examples: float32 [2048, 32768], P(('grp', 'dev'))
- labels: int32 [2048], P(('grp', 'dev')), may hold values from 0 to 1, as said below
Outputs:
- consensus: float32 [32768], replicated
- local_weights: float32 [32, 32768], P(('grp', 'dev'))
- dual_vars: float32 [32, 32768], P(('grp', 'dev'))
Inputs may be any that keep to these rules, and one draw needn't show every extreme that they name: `labels`: each example's class, 0 or 1.
All inputs are finite; a program needn't handle non-finite values.
Results may differ from a plain program's by a relative error of at most 0.00012.
Values sent between devices are 32-bit elements; how exact they have to be, the bound alone decides.
A program may use at most 64 MiB of HBM per device.

v0:
```python
import jax
import jax.numpy as jnp
from jax import lax
from jax.sharding import PartitionSpec as P

PROX = 3
ROUNDS = 4
step_size = 200.0
penalty = 0.005
thresh = 0.04


def shrink(values):
    return values - jnp.clip(values, -thresh, thresh)


def local_steps(examples, targets, weight_vector, consensus_point):
    for prox_index in range(PROX):
        label_margins = jnp.dot(examples, weight_vector, precision=lax.Precision.HIGHEST)
        primal_residual = jax.nn.sigmoid(label_margins) - targets
        loss_gradient = jnp.dot(primal_residual, examples, precision=lax.Precision.HIGHEST)
        weight_vector = (
            weight_vector - step_size * loss_gradient + step_size * penalty * consensus_point
        ) / (1.0 + step_size * penalty)
    return weight_vector


def per_device(examples, labels):
    members = lax.axis_size("grp") * lax.axis_size("dev")
    targets = labels.astype(jnp.float32)
    width = examples.shape[1]

    def one_round(round_index, carried):
        consensus, weight_vector, dual_vars = carried
        consensus_point = consensus - dual_vars
        weight_vector = local_steps(examples, targets, weight_vector, consensus_point)
        combined = weight_vector + dual_vars
        summed = lax.psum(combined, ("grp", "dev"))
        consensus = shrink(summed / members)
        dual_vars = dual_vars + weight_vector - consensus
        return (consensus, weight_vector, dual_vars)

    start = (
        jnp.zeros((width,), jnp.float32),
        jnp.zeros((width,), jnp.float32),
        jnp.zeros((width,), jnp.float32),
    )
    consensus, weight_vector, dual_vars = lax.fori_loop(0, ROUNDS, one_round, start)
    return (consensus, weight_vector[None, :], dual_vars[None, :])


def solution(mesh):
    placed = (P(("grp", "dev"), None), P(("grp", "dev")))
    return jax.shard_map(
        per_device,
        mesh=mesh,
        in_specs=placed,
        out_specs=(P(), P(("grp", "dev"), None), P(("grp", "dev"), None)),
        check_vma=False,
    )
```

profile of v0, /device:TPU:0, one launch (start us, length us, event | category | flops | bytes accessed | tf_op | source)
XLA Modules:
  0.0 658.6 jit_solution(14624794344501646285)
XLA Ops:
  7.8 643.4 %while.15 = (s32[]{:T(128)}, f32[32768]{0:T(1024)S(1)}, f32[32768]{0:T(1024)S(1)}, f32[32768]{0:T(1024)S(1)}, f32[64,32768]{1,0:T(8,128)}, /*index=5*/f32[64]{0:T(128)S(1)}, s32[]{:T(128)}, s32[]{:T(128)}) while((s32[]{:T(128)}, f32[32768]{0:T(1024)S(1)}, f32[32768]{0:T(1024)S(1)}, f32[32768]{0:T(1024)S(1)}, ...), condition=%wide.region_2.3_spmd.clone, body=%wide.region_0.2_spmd.clone.sunk | while | flops 151782144 | bytes 88344992 | solution.py:48
  7.9 9.1 %fusion.65 = f32[64,1]{0,1:T(1,128)S(1)} fusion(f32[64]{0:T(128)S(1)} %get-tuple-element.149, f32[64,32768]{1,0:T(8,128)} %get-tuple-element.148, f32[32768,1]{0,1:T(1,128)S(1)} %bitcast.118), kind=kOutput, calls=%fused_computation.20.clone.1 | convolution fusion | flops 25166080 | bytes 8520192 | tf_op jit(solution)/shard_map/while/body/eval_jaxpr/dot_general | solution.py:19
  16.9 4.0 fusion.66
  21.0 6.6 fusion.67
  27.6 4.1 fusion.68
  31.7 6.6 fusion.69
  38.3 4.1 fusion.70
  43.0 127.3 %all-reduce.2.cloned.1.call-done = f32[32768]{0:T(1024)} async-done(((f32[32768]{0:T(1024)}), f32[32768]{0:T(1024)}) %all-reduce.2.cloned.1.call-update) | async-done | bytes 131088 | tf_op jit(solution)/shard_map/while/body/eval_jaxpr/psum | solution.py:38
  170.4 1.0 fusion.71
  171.5 9.1 %fusion.65 = f32[64,1]{0,1:T(1,128)S(1)} fusion(f32[64]{0:T(128)S(1)} %get-tuple-element.149, f32[64,32768]{1,0:T(8,128)} %get-tuple-element.148, f32[32768,1]{0,1:T(1,128)S(1)} %bitcast.118), kind=kOutput, calls=%fused_computation.20.clone.1 | convolution fusion | flops 25166080 | bytes 8520192 | tf_op jit(solution)/shard_map/while/body/eval_jaxpr/dot_general | solution.py:19
  180.5 4.0 fusion.66
  184.6 6.6 fusion.67
  191.2 4.1 fusion.68
  195.3 6.6 fusion.69
  201.9 4.1 fusion.70
  206.6 123.7 %all-reduce.2.cloned.1.call-done = f32[32768]{0:T(1024)} async-done(((f32[32768]{0:T(1024)}), f32[32768]{0:T(1024)}) %all-reduce.2.cloned.1.call-update) | async-done | bytes 131088 | tf_op jit(solution)/shard_map/while/body/eval_jaxpr/psum | solution.py:38
  330.3 1.0 fusion.71
  331.4 9.1 %fusion.65 = f32[64,1]{0,1:T(1,128)S(1)} fusion(f32[64]{0:T(128)S(1)} %get-tuple-element.149, f32[64,32768]{1,0:T(8,128)} %get-tuple-element.148, f32[32768,1]{0,1:T(1,128)S(1)} %bitcast.118), kind=kOutput, calls=%fused_computation.20.clone.1 | convolution fusion | flops 25166080 | bytes 8520192 | tf_op jit(solution)/shard_map/while/body/eval_jaxpr/dot_general | solution.py:19
  340.5 4.0 fusion.66
  344.6 6.6 fusion.67
  351.2 4.1 fusion.68
  355.3 6.6 fusion.69
  361.8 4.1 fusion.70
  366.6 123.7 %all-reduce.2.cloned.1.call-done = f32[32768]{0:T(1024)} async-done(((f32[32768]{0:T(1024)}), f32[32768]{0:T(1024)}) %all-reduce.2.cloned.1.call-update) | async-done | bytes 131088 | tf_op jit(solution)/shard_map/while/body/eval_jaxpr/psum | solution.py:38
  490.3 1.0 fusion.71
  491.4 9.1 %fusion.65 = f32[64,1]{0,1:T(1,128)S(1)} fusion(f32[64]{0:T(128)S(1)} %get-tuple-element.149, f32[64,32768]{1,0:T(8,128)} %get-tuple-element.148, f32[32768,1]{0,1:T(1,128)S(1)} %bitcast.118), kind=kOutput, calls=%fused_computation.20.clone.1 | convolution fusion | flops 25166080 | bytes 8520192 | tf_op jit(solution)/shard_map/while/body/eval_jaxpr/dot_general | solution.py:19
  500.5 4.0 fusion.66
  504.6 6.6 fusion.67
  511.1 4.1 fusion.68
  515.2 6.6 fusion.69
  521.8 4.1 fusion.70
  526.6 123.7 %all-reduce.2.cloned.1.call-done = f32[32768]{0:T(1024)} async-done(((f32[32768]{0:T(1024)}), f32[32768]{0:T(1024)}) %all-reduce.2.cloned.1.call-update) | async-done | bytes 131088 | tf_op jit(solution)/shard_map/while/body/eval_jaxpr/psum | solution.py:38
  (43 shorter events, 5.7 us)
Async XLA Ops:
  7.8 162.5 %all-reduce.2.cloned.1.call-start = ((), (), s32[]{:S(2)}) async-start(), calls=%async_computation | async-start | bytes 262144 | tf_op jit(solution)/shard_map/while/body/eval_jaxpr/psum | solution.py:38
  7.8 9.1 %copy-start = (f32[64,32768]{1,0:T(8,128)S(1)}, f32[64,32768]{1,0:T(8,128)}, u32[]{:S(2)}) copy-start(f32[64,32768]{1,0:T(8,128)} %get-tuple-element.148) | copy-start | bytes 25165828 | tf_op jit(solution)/shard_map/while
  171.4 159.0 %all-reduce.2.cloned.1.call-start = ((), (), s32[]{:S(2)}) async-start(), calls=%async_computation | async-start | bytes 262144 | tf_op jit(solution)/shard_map/while/body/eval_jaxpr/psum | solution.py:38
  171.4 9.1 %copy-start = (f32[64,32768]{1,0:T(8,128)S(1)}, f32[64,32768]{1,0:T(8,128)}, u32[]{:S(2)}) copy-start(f32[64,32768]{1,0:T(8,128)} %get-tuple-element.148) | copy-start | bytes 25165828 | tf_op jit(solution)/shard_map/while
  331.3 159.0 %all-reduce.2.cloned.1.call-start = ((), (), s32[]{:S(2)}) async-start(), calls=%async_computation | async-start | bytes 262144 | tf_op jit(solution)/shard_map/while/body/eval_jaxpr/psum | solution.py:38
  331.4 9.1 %copy-start = (f32[64,32768]{1,0:T(8,128)S(1)}, f32[64,32768]{1,0:T(8,128)}, u32[]{:S(2)}) copy-start(f32[64,32768]{1,0:T(8,128)} %get-tuple-element.148) | copy-start | bytes 25165828 | tf_op jit(solution)/shard_map/while
  491.3 159.0 %all-reduce.2.cloned.1.call-start = ((), (), s32[]{:S(2)}) async-start(), calls=%async_computation | async-start | bytes 262144 | tf_op jit(solution)/shard_map/while/body/eval_jaxpr/psum | solution.py:38
  491.4 9.1 %copy-start = (f32[64,32768]{1,0:T(8,128)S(1)}, f32[64,32768]{1,0:T(8,128)}, u32[]{:S(2)}) copy-start(f32[64,32768]{1,0:T(8,128)} %get-tuple-element.148) | copy-start | bytes 25165828 | tf_op jit(solution)/shard_map/while
  651.3 0.7 copy-start.1
  651.3 0.7 copy-start.2
  651.3 0.7 copy-start.3
Sparse Core Ops, SparseCore 0:
  43.2 127.1 all-reduce.1
  206.8 123.5 all-reduce.1
  366.7 123.5 all-reduce.1
  526.7 123.5 all-reduce.1
where the time goes:
time: 659 us
  waiting for transfers between devices  498 us (76%)
  matrix products  137 us (21%)
  between operations  13.7 us (2%)
  other arithmetic  7.74 us (1%)
    psum x4, waiting for transfers between devices, one_round(): summed = lax.psum(combined, ('grp', 'dev'))  498 us
    dot_general x12, matrix products, local_steps(): jnp.dot(examples, weight_vector, precision=lax.Precision.HIGHEST)  88.9 us
    dot_general x12, matrix products, local_steps(): jnp.dot(primal_residual, examples, precision=lax.Precision.HIGHEST)  48.6 us
  transfers between devices with their start and end apart: 4, of which 4 were waited for; matrix products, arithmetic and copies ran while one was open for 0% of the time, Pallas kernels for 0%

commit v1 on v0

--- a/solution.py
+++ b/solution.py
@@ -1,13 +1,22 @@
+import functools
 import jax
 import jax.numpy as jnp
 from jax import lax
 from jax.sharding import PartitionSpec as P
+from jax.lax import all_gather
 
 PROX = 3
 ROUNDS = 4
 step_size = 200.0
 penalty = 0.005
 thresh = 0.04
+
+
+def _edit_ways(raw, a_name):
+    return jnp.sum(all_gather(raw, a_name), 0)
+
+
+scenes_keep_up = functools.partial(_edit_ways, a_name=("grp", "dev"))
 
 
 def shrink(values):
@@ -35,7 +44,7 @@
         consensus_point = consensus - dual_vars
         weight_vector = local_steps(examples, targets, weight_vector, consensus_point)
         combined = weight_vector + dual_vars
-        summed = lax.psum(combined, ("grp", "dev"))
+        summed = scenes_keep_up(combined)
         consensus = shrink(summed / members)
         dual_vars = dual_vars + weight_vector - consensus
         return (consensus, weight_vector, dual_vars)

time: 659 us -> 434 us (0.66)
  waiting for transfers between devices: 498 us -> 246 us
  local copies, waits for them, and re-layouts: 0.75 us -> 20.6 us
    psum x4 -> x0, waiting for transfers between devices: 498 us -> none  [one_round(): summed = lax.psum(combined, ('grp', 'dev'))]
    all_gather x0 -> x4, waiting for transfers between devices: none -> 246 us  [_edit_ways(): return jnp.sum(all_gather(raw, a_name), 0)]
    all_gather x0 -> x4, local copies, waits for them, and re-layouts: none -> 19.9 us  [_edit_ways(): return jnp.sum(all_gather(raw, a_name), 0)]
    reduce_sum x0 -> x4, other arithmetic: none -> 10.4 us  [_edit_ways(): return jnp.sum(all_gather(raw, a_name), 0)]
where the time goes in v1:
time: 434 us; the launch traced here: 433 us
  waiting for transfers between devices  246 us (57%)
  matrix products  137 us (32%)
  local copies, waits for them, and re-layouts  20.6 us (5%)
  other arithmetic  14.3 us (3%)
  between operations  13.7 us (3%)
    all_gather x4, waiting for transfers between devices, _edit_ways(): return jnp.sum(all_gather(raw, a_name), 0)  246 us
    dot_general x12, matrix products, local_steps(): jnp.dot(examples, weight_vector, precision=lax.Precision.HIGHEST)  88.9 us
    dot_general x12, matrix products, local_steps(): jnp.dot(primal_residual, examples, precision=lax.Precision.HIGHEST)  48.6 us
    all_gather x4, local copies, waits for them, and re-layouts, _edit_ways(): return jnp.sum(all_gather(raw, a_name), 0)  19.9 us
    reduce_sum x4, other arithmetic, _edit_ways(): return jnp.sum(all_gather(raw, a_name), 0)  10.4 us
  transfers between devices with their start and end apart: 4, of which 4 were waited for; matrix products, arithmetic and copies ran while one was open for 0% of the time, Pallas kernels for 0%

profile of v1, /device:TPU:0, one launch (start us, length us, event | category | flops | bytes accessed | tf_op | source)
XLA Modules:
  0.0 433.0 jit_solution(9894575466883503148)
XLA Ops:
  7.8 417.9 %while.15 = (s32[]{:T(128)}, f32[32768]{0:T(1024)S(1)}, f32[32768]{0:T(1024)S(1)}, f32[32768]{0:T(1024)S(1)}, f32[64,32768]{1,0:T(8,128)}, /*index=5*/f32[64]{0:T(128)S(1)}, s32[]{:T(128)}, s32[]{:T(128)}, f32[]{:T(128)}) while((s32[]{:T(128)}, f32[32768]{0:T(1024)S(1)}, f32[32768]{0:T(1024)S(1)}, f32[32768]{0:T(1024)S(1)}, ...), condition=%wide.region_2.3_spmd.clone, body=%wide.region_0.2_spmd.clone.sunk | while | flops 152765184 | bytes 113772992 | solution.py:57
  7.9 9.1 %fusion.65 = f32[64,1]{0,1:T(1,128)S(1)} fusion(f32[64]{0:T(128)S(1)} %get-tuple-element.151, f32[64,32768]{1,0:T(8,128)} %get-tuple-element.150, f32[32768,1]{0,1:T(1,128)S(1)} %bitcast.118), kind=kOutput, calls=%fused_computation.20.clone.1 | convolution fusion | flops 25166080 | bytes 8520192 | tf_op jit(solution)/shard_map/while/body/eval_jaxpr/dot_general | solution.py:28
  16.9 4.0 fusion.66
  21.0 6.6 %fusion.67 = f32[64,1]{0,1:T(1,128)S(1)} fusion(f32[64]{0:T(128)S(1)} %get-tuple-element.151, f32[32768,1]{0,1:T(1,128)S(1)} %bitcast.117, f32[64,32768]{1,0:T(8,128)S(1)} %copy-done), kind=kOutput, calls=%fused_computation.13.clone.1 | convolution fusion | flops 25166080 | bytes 8520192 | tf_op jit(solution)/shard_map/while/body/eval_jaxpr/dot_general | solution.py:28
  27.6 4.1 fusion.68
  31.7 6.6 %fusion.69 = f32[64,1]{0,1:T(1,128)S(1)} fusion(f32[64]{0:T(128)S(1)} %get-tuple-element.151, f32[32768,1]{0,1:T(1,128)S(1)} %bitcast.116, f32[64,32768]{1,0:T(8,128)S(1)} %copy-done), kind=kOutput, calls=%fused_computation.6.clone.1 | convolution fusion | flops 25166080 | bytes 8520192 | tf_op jit(solution)/shard_map/while/body/eval_jaxpr/dot_general | solution.py:28
  38.3 4.1 fusion.70
  43.0 64.5 %all-gather.6.cloned.1.call-done = f32[1048576]{0:T(1024)} async-done(((f32[32768]{0:T(1024)}), f32[1048576]{0:T(1024)}) %all-gather.6.cloned.1.call-update) | async-done | bytes 4194320 | tf_op jit(solution)/shard_map/while/body/eval_jaxpr/all_gather | solution.py:16
  107.6 5.0 %reshape.21 = f32[32,32768]{1,0:T(8,128)} reshape(f32[1048576]{0:T(1024)} %all-gather.6.cloned.1.call-done) | data formatting | bytes 8388608 | tf_op jit(solution)/shard_map/while/body/eval_jaxpr/all_gather | solution.py:16
  115.3 9.1 %fusion.65 = f32[64,1]{0,1:T(1,128)S(1)} fusion(f32[64]{0:T(128)S(1)} %get-tuple-element.151, f32[64,32768]{1,0:T(8,128)} %get-tuple-element.150, f32[32768,1]{0,1:T(1,128)S(1)} %bitcast.118), kind=kOutput, calls=%fused_computation.20.clone.1 | convolution fusion | flops 25166080 | bytes 8520192 | tf_op jit(solution)/shard_map/while/body/eval_jaxpr/dot_general | solution.py:28
  124.4 4.0 fusion.66
  128.5 6.6 %fusion.67 = f32[64,1]{0,1:T(1,128)S(1)} fusion(f32[64]{0:T(128)S(1)} %get-tuple-element.151, f32[32768,1]{0,1:T(1,128)S(1)} %bitcast.117, f32[64,32768]{1,0:T(8,128)S(1)} %copy-done), kind=kOutput, calls=%fused_computation.13.clone.1 | convolution fusion | flops 25166080 | bytes 8520192 | tf_op jit(solution)/shard_map/while/body/eval_jaxpr/dot_general | solution.py:28
  135.1 4.1 fusion.68
  139.1 6.6 %fusion.69 = f32[64,1]{0,1:T(1,128)S(1)} fusion(f32[64]{0:T(128)S(1)} %get-tuple-element.151, f32[32768,1]{0,1:T(1,128)S(1)} %bitcast.116, f32[64,32768]{1,0:T(8,128)S(1)} %copy-done), kind=kOutput, calls=%fused_computation.6.clone.1 | convolution fusion | flops 25166080 | bytes 8520192 | tf_op jit(solution)/shard_map/while/body/eval_jaxpr/dot_general | solution.py:28
  145.7 4.1 fusion.70
  150.5 60.6 %all-gather.6.cloned.1.call-done = f32[1048576]{0:T(1024)} async-done(((f32[32768]{0:T(1024)}), f32[1048576]{0:T(1024)}) %all-gather.6.cloned.1.call-update) | async-done | bytes 4194320 | tf_op jit(solution)/shard_map/while/body/eval_jaxpr/all_gather | solution.py:16
  211.1 5.0 %reshape.21 = f32[32,32768]{1,0:T(8,128)} reshape(f32[1048576]{0:T(1024)} %all-gather.6.cloned.1.call-done) | data formatting | bytes 8388608 | tf_op jit(solution)/shard_map/while/body/eval_jaxpr/all_gather | solution.py:16
  218.8 9.1 %fusion.65 = f32[64,1]{0,1:T(1,128)S(1)} fusion(f32[64]{0:T(128)S(1)} %get-tuple-element.151, f32[64,32768]{1,0:T(8,128)} %get-tuple-element.150, f32[32768,1]{0,1:T(1,128)S(1)} %bitcast.118), kind=kOutput, calls=%fused_computation.20.clone.1 | convolution fusion | flops 25166080 | bytes 8520192 | tf_op jit(solution)/shard_map/while/body/eval_jaxpr/dot_general | solution.py:28
  227.9 4.0 fusion.66
  232.0 6.6 %fusion.67 = f32[64,1]{0,1:T(1,128)S(1)} fusion(f32[64]{0:T(128)S(1)} %get-tuple-element.151, f32[32768,1]{0,1:T(1,128)S(1)} %bitcast.117, f32[64,32768]{1,0:T(8,128)S(1)} %copy-done), kind=kOutput, calls=%fused_computation.13.clone.1 | convolution fusion | flops 25166080 | bytes 8520192 | tf_op jit(solution)/shard_map/while/body/eval_jaxpr/dot_general | solution.py:28
  238.6 4.1 fusion.68
  242.7 6.6 %fusion.69 = f32[64,1]{0,1:T(1,128)S(1)} fusion(f32[64]{0:T(128)S(1)} %get-tuple-element.151, f32[32768,1]{0,1:T(1,128)S(1)} %bitcast.116, f32[64,32768]{1,0:T(8,128)S(1)} %copy-done), kind=kOutput, calls=%fused_computation.6.clone.1 | convolution fusion | flops 25166080 | bytes 8520192 | tf_op jit(solution)/shard_map/while/body/eval_jaxpr/dot_general | solution.py:28
  249.2 4.1 fusion.70
  254.0 60.6 %all-gather.6.cloned.1.call-done = f32[1048576]{0:T(1024)} async-done(((f32[32768]{0:T(1024)}), f32[1048576]{0:T(1024)}) %all-gather.6.cloned.1.call-update) | async-done | bytes 4194320 | tf_op jit(solution)/shard_map/while/body/eval_jaxpr/all_gather | solution.py:16
  314.6 5.0 %reshape.21 = f32[32,32768]{1,0:T(8,128)} reshape(f32[1048576]{0:T(1024)} %all-gather.6.cloned.1.call-done) | data formatting | bytes 8388608 | tf_op jit(solution)/shard_map/while/body/eval_jaxpr/all_gather | solution.py:16
  322.3 9.1 %fusion.65 = f32[64,1]{0,1:T(1,128)S(1)} fusion(f32[64]{0:T(128)S(1)} %get-tuple-element.151, f32[64,32768]{1,0:T(8,128)} %get-tuple-element.150, f32[32768,1]{0,1:T(1,128)S(1)} %bitcast.118), kind=kOutput, calls=%fused_computation.20.clone.1 | convolution fusion | flops 25166080 | bytes 8520192 | tf_op jit(solution)/shard_map/while/body/eval_jaxpr/dot_general | solution.py:28
  335.5 6.6 %fusion.67 = f32[64,1]{0,1:T(1,128)S(1)} fusion(f32[64]{0:T(128)S(1)} %get-tuple-element.151, f32[32768,1]{0,1:T(1,128)S(1)} %bitcast.117, f32[64,32768]{1,0:T(8,128)S(1)} %copy-done), kind=kOutput, calls=%fused_computation.13.clone.1 | convolution fusion | flops 25166080 | bytes 8520192 | tf_op jit(solution)/shard_map/while/body/eval_jaxpr/dot_general | solution.py:28
  342.1 4.1 fusion.68
  346.2 6.6 %fusion.69 = f32[64,1]{0,1:T(1,128)S(1)} fusion(f32[64]{0:T(128)S(1)} %get-tuple-element.151, f32[32768,1]{0,1:T(1,128)S(1)} %bitcast.116, f32[64,32768]{1,0:T(8,128)S(1)} %copy-done), kind=kOutput, calls=%fused_computation.6.clone.1 | convolution fusion | flops 25166080 | bytes 8520192 | tf_op jit(solution)/shard_map/while/body/eval_jaxpr/dot_general | solution.py:28
  352.7 4.1 fusion.70
  357.5 60.6 %all-gather.6.cloned.1.call-done = f32[1048576]{0:T(1024)} async-done(((f32[32768]{0:T(1024)}), f32[1048576]{0:T(1024)}) %all-gather.6.cloned.1.call-update) | async-done | bytes 4194320 | tf_op jit(solution)/shard_map/while/body/eval_jaxpr/all_gather | solution.py:16
  418.1 5.0 %reshape.21 = f32[32,32768]{1,0:T(8,128)} reshape(f32[1048576]{0:T(1024)} %all-gather.6.cloned.1.call-done) | data formatting | bytes 8388608 | tf_op jit(solution)/shard_map/while/body/eval_jaxpr/all_gather | solution.py:16
  (59 shorter events, 19.2 us)
Async XLA Ops:
  7.8 99.8 %all-gather.6.cloned.1.call-start = ((), (), s32[]{:S(2)}) async-start(), calls=%async_computation | async-start | bytes 4325376 | tf_op jit(solution)/shard_map/while/body/eval_jaxpr/all_gather | solution.py:16
  7.8 9.1 %copy-start = (f32[64,32768]{1,0:T(8,128)S(1)}, f32[64,32768]{1,0:T(8,128)}, u32[]{:S(2)}) copy-start(f32[64,32768]{1,0:T(8,128)} %get-tuple-element.150) | copy-start | bytes 25165828 | tf_op jit(solution)/shard_map/while
  43.0 72.2 %copy-start.1 = (f32[32768]{0:T(1024)S(1)}, f32[32768]{0:T(1024)}, u32[]{:S(2)}) copy-start(f32[32768]{0:T(1024)} %get-tuple-element.124) | copy-start | bytes 393220 | tf_op jit(solution)/shard_map/while
  115.2 95.9 %all-gather.6.cloned.1.call-start = ((), (), s32[]{:S(2)}) async-start(), calls=%async_computation | async-start | bytes 4325376 | tf_op jit(solution)/shard_map/while/body/eval_jaxpr/all_gather | solution.py:16
  115.3 9.1 %copy-start = (f32[64,32768]{1,0:T(8,128)S(1)}, f32[64,32768]{1,0:T(8,128)}, u32[]{:S(2)}) copy-start(f32[64,32768]{1,0:T(8,128)} %get-tuple-element.150) | copy-start | bytes 25165828 | tf_op jit(solution)/shard_map/while
  150.5 68.2 %copy-start.1 = (f32[32768]{0:T(1024)S(1)}, f32[32768]{0:T(1024)}, u32[]{:S(2)}) copy-start(f32[32768]{0:T(1024)} %get-tuple-element.124) | copy-start | bytes 393220 | tf_op jit(solution)/shard_map/while
  218.7 95.9 %all-gather.6.cloned.1.call-start = ((), (), s32[]{:S(2)}) async-start(), calls=%async_computation | async-start | bytes 4325376 | tf_op jit(solution)/shard_map/while/body/eval_jaxpr/all_gather | solution.py:16
  218.8 9.1 %copy-start = (f32[64,32768]{1,0:T(8,128)S(1)}, f32[64,32768]{1,0:T(8,128)}, u32[]{:S(2)}) copy-start(f32[64,32768]{1,0:T(8,128)} %get-tuple-element.150) | copy-start | bytes 25165828 | tf_op jit(solution)/shard_map/while
  254.0 68.2 %copy-start.1 = (f32[32768]{0:T(1024)S(1)}, f32[32768]{0:T(1024)}, u32[]{:S(2)}) copy-start(f32[32768]{0:T(1024)} %get-tuple-element.124) | copy-start | bytes 393220 | tf_op jit(solution)/shard_map/while
  322.2 95.9 %all-gather.6.cloned.1.call-start = ((), (), s32[]{:S(2)}) async-start(), calls=%async_computation | async-start | bytes 4325376 | tf_op jit(solution)/shard_map/while/body/eval_jaxpr/all_gather | solution.py:16
  322.3 9.1 %copy-start = (f32[64,32768]{1,0:T(8,128)S(1)}, f32[64,32768]{1,0:T(8,128)}, u32[]{:S(2)}) copy-start(f32[64,32768]{1,0:T(8,128)} %get-tuple-element.150) | copy-start | bytes 25165828 | tf_op jit(solution)/shard_map/while
  357.5 68.2 %copy-start.1 = (f32[32768]{0:T(1024)S(1)}, f32[32768]{0:T(1024)}, u32[]{:S(2)}) copy-start(f32[32768]{0:T(1024)} %get-tuple-element.124) | copy-start | bytes 393220 | tf_op jit(solution)/shard_map/while
  425.8 0.7 copy-start.2
  425.8 0.7 copy-start.3
  425.8 0.7 copy-start.4
Sparse Core Ops, SparseCore 0:
  43.2 64.3 all-gather.5
  150.6 60.4 all-gather.5
  254.1 60.4 all-gather.5
  357.6 60.4 all-gather.5
